TPU v7x, 256 devices: a whole 4x4x8 slice. The times are simulated.
256 devices in a mesh: gx: 4 (over x), gy: 8 (over y, core), gz: 8 (over z).
Axes of the slice: x: 4, y: 4, z: 8, core: 2. Of those that a mesh axis runs over, the one named last changes fastest.
Arguments:
- right_side: float32 [8, 32, 256, 1024], P(None, 'gx', 'gy', 'gz'), may hold values from -12 to 12
- shift: float32 [32, 256, 1024], P('gx', 'gy', 'gz'), may hold values from 0.02 to 2
Outputs:
- solution_block: float32 [8, 32, 256, 1024], P(None, 'gx', 'gy', 'gz')
- residual_norms: float32 [8], replicated
All inputs are finite; a program needn't handle non-finite values.
Results may differ from a plain program's by a relative error of at most 0.0003.
Values sent between devices are 32-bit elements; how exact they have to be, the bound alone decides.
A program may use at most 128 MiB of HBM per device.

v0:
```python
import jax
import jax.numpy as jnp
from jax import lax
from jax.sharding import Mesh
from jax.sharding import PartitionSpec as P

ITERS = 2
GX_GY_GZ = ("gx", "gy_0", "gy_1", "gz")
GY = ("gy_0", "gy_1")


def padded_2(value, sides, width):
    edges = {}
    for axis, dim in sides:
        devices, length = (lax.axis_size(axis), value.shape[dim])
        up = [(i, (i + 1) % devices) for i in range(devices - 1)]
        last = lax.slice_in_dim(value, length - width, length, axis=dim)
        leading = lax.slice_in_dim(value, 0, width, axis=dim)
        edges[dim] = (
            lax.ppermute(last, axis, up),
            lax.ppermute(leading, axis, [(b, a) for a, b in up]),
        )
    done = []
    for _, dim in sides:
        low, high = edges[dim]
        around = [(width, width) if d in done else (0, 0) for d in range(value.ndim)]
        value = jnp.concatenate([jnp.pad(low, around), value, jnp.pad(high, around)], axis=dim)
        done.append(dim)
    return value


def by_axis(value, axes):
    for axis in axes:
        value = lax.psum(value, axis)
    return value


def operate(fields, shift):
    padded = padded_2(fields, (("gx", 1), (GY, 2), ("gz", 3)), 1)
    beside = padded[:, 2:, 1:-1, 1:-1] + padded[:, :-2, 1:-1, 1:-1]
    beside = beside + padded[:, 1:-1, 2:, 1:-1] + padded[:, 1:-1, :-2, 1:-1]
    beside = beside + padded[:, 1:-1, 1:-1, 2:] + padded[:, 1:-1, 1:-1, :-2]
    return (6.0 + shift)[None] * fields - beside


def lower_inverse(lower):
    count = lower.shape[0]
    return jax.scipy.linalg.solve_triangular(lower, jnp.eye(count, dtype=lower.dtype), lower=True)


def small_dot(left, right):
    return jnp.dot(left, right, precision=lax.Precision.HIGHEST)


def body(right_side, shift):
    width = right_side.shape[0]
    shape = right_side.shape
    rows = right_side.reshape(width, -1)
    first_step = None
    images = operate(right_side, shift).reshape(width, -1)
    both = jnp.concatenate([rows, images], axis=0)
    joint = by_axis(small_dot(both, both.T), GX_GY_GZ)
    lower = jnp.linalg.cholesky(joint[:width, :width])
    start_coeff = lower.T
    inverse = lower_inverse(lower)
    first_basis = small_dot(inverse, rows)
    basis = [first_basis]
    first_image = small_dot(inverse, images)
    first_coeffs = small_dot(small_dot(inverse, joint[:width, width:]), inverse.T)
    first_self = small_dot(small_dot(inverse, joint[width:, width:]), inverse.T)
    first_gram = first_self - small_dot(first_coeffs.T, first_coeffs)
    first_projected = first_image - small_dot(first_coeffs.T, first_basis)
    first_step = (first_coeffs, first_gram, first_projected)
    hessen = jnp.zeros(((ITERS + 1) * width, ITERS * width), jnp.float32)
    for step in range(ITERS):
        if step == 0 and first_step is not None:
            coeffs, gram, projected = first_step
        else:
            image = operate(basis[step].reshape(shape), shift).reshape(width, -1)
            stacked = jnp.concatenate(basis, axis=0)
            products = by_axis(
                small_dot(jnp.concatenate([stacked, image], axis=0), image.T), GX_GY_GZ
            )
            coeffs = products[:-width]
            gram = products[-width:] - small_dot(coeffs.T, coeffs)
            projected = image - small_dot(coeffs.T, stacked)
        lower = jnp.linalg.cholesky(gram)
        hessen = hessen.at[: (step + 1) * width, step * width : (step + 1) * width].set(coeffs)
        hessen = hessen.at[
            (step + 1) * width : (step + 2) * width, step * width : (step + 1) * width
        ].set(lower.T)
        if step + 1 < ITERS:
            basis.append(small_dot(lower_inverse(lower), projected))
    target = jnp.zeros(((ITERS + 1) * width, width), jnp.float32).at[:width].set(start_coeff)
    normal = small_dot(hessen.T, hessen)
    factor = jnp.linalg.cholesky(normal)
    coeff_y = jax.scipy.linalg.cho_solve((factor, True), small_dot(hessen.T, target))
    solution = small_dot(coeff_y.T, jnp.concatenate(basis, axis=0)).reshape(shape)
    leftover = target - small_dot(hessen, coeff_y)
    norms = jnp.sqrt(jnp.sum(leftover * leftover, axis=0))
    return (solution, norms)


def solution(mesh):
    split = Mesh(
        mesh.devices.reshape(mesh.shape["gx"], 4, 2, mesh.shape["gz"]), ("gx", "gy_0", "gy_1", "gz")
    )
    return jax.shard_map(
        body,
        mesh=split,
        in_specs=(P(None, "gx", GY, "gz"), P("gx", GY, "gz")),
        out_specs=(P(None, "gx", GY, "gz"), P()),
        check_vma=False,
    )
```

profile of v0, /device:TPU:8, one launch (start us, length us, event | category | flops | bytes accessed | tf_op | source)
XLA Modules:
  0.0 174.2 jit_solution(10873587700840309843)
XLA Ops:
  0.6 1.7 fusion.68
  2.3 3.4 %collective-permute-start.1 = (f32[8,1,32,128]{3,2,1,0:T(8,128)}, f32[8,1,32,128]{3,2,1,0:T(8,128)S(1)}, u32[]{:S(2)}, u32[]{:S(2)}) collective-permute-start(f32[8,1,32,128]{3,2,1,0:T(8,128)} %get-tuple-element.79), channel_id=1, source_target_pairs={{0,64},{64,128},{128,192},{1,65},{65,129},{129,193},{2,66},{66,130... | collective-permute-start | bytes 393224 | tf_op jit(solution)/shard_map/ppermute | solution.py:20
  5.7 1.9 %fusion.66 = (f32[8,8,32,1]{3,2,1,0:T(8,128)S(1)}, f32[8,8,32,1]{3,2,1,0:T(8,128)S(1)}) fusion(f32[8,8,32,128]{3,2,1,0:T(8,128)} %param.15), kind=kLoop, calls=%fused_computation.126 | loop fusion | bytes 32768 | tf_op jit(solution)/shard_map/slice | solution.py:18
  7.7 1.0 copy.56
  8.7 1.3 collective-permute-start.4
  10.0 1.0 copy.57
  11.0 4.7 %collective-permute-start.5 = (f32[8,8,32,1]{2,1,3,0:T(8,128)}, f32[8,8,32,1]{2,1,3,0:T(8,128)S(1)}, u32[]{:S(2)}, u32[]{:S(2)}) collective-permute-start(f32[8,8,32,1]{2,1,3,0:T(8,128)} %copy.57), channel_id=1, source_target_pairs={{0,1},{1,2},{2,3},{3,4},{4,5},{5,6},{6,7},{8,9},{9,10},{10,11},{11... | collective-permute-start | bytes 24584 | tf_op jit(solution)/shard_map/ppermute | solution.py:20
  15.8 1.9 %collective-permute-start.2 = (f32[8,8,1,128]{3,2,1,0:T(1,128)S(1)}, f32[8,8,1,128]{3,2,1,0:T(1,128)S(1)}, u32[]{:S(2)}, u32[]{:S(2)}) collective-permute-start(f32[8,8,1,128]{3,2,1,0:T(1,128)S(1)} %get-tuple-element.77), channel_id=1, source_target_pairs={{8,0},{16,8},{24,16},{32,24},{40,32},{48,40},{56,48},{9,1},{17,9},... | collective-permute-start | bytes 98312 | tf_op jit(solution)/shard_map/ppermute | solution.py:21
  17.7 2.4 %collective-permute-start.3 = (f32[8,8,1,128]{3,2,1,0:T(1,128)S(1)}, f32[8,8,1,128]{3,2,1,0:T(1,128)S(1)}, u32[]{:S(2)}, u32[]{:S(2)}) collective-permute-start(f32[8,8,1,128]{3,2,1,0:T(1,128)S(1)} %get-tuple-element.76), channel_id=1, source_target_pairs={{0,8},{8,16},{16,24},{24,32},{32,40},{40,48},{48,56},{1,9},{9,17},... | collective-permute-start | bytes 98312 | tf_op jit(solution)/shard_map/ppermute | solution.py:20
  20.8 1.3 collective-permute-start
  22.1 2.2 %copy.60 = f32[8,8,32,1]{3,2,1,0:T(8,128)} copy(f32[8,8,32,1]{2,1,3,0:T(8,128)} %collective-permute-done.4) | data formatting | bytes 16384
  24.3 1.4 copy.61
  25.9 2.9 %collective-permute-done = f32[8,1,32,128]{3,2,1,0:T(8,128)S(1)} collective-permute-done((f32[8,1,32,128]{3,2,1,0:T(8,128)S(1)}, f32[8,1,32,128]{3,2,1,0:T(8,128)S(1)}, u32[]{:S(2)}, u32[]{:S(2)}) %collective-permute-start) | collective-permute-done | bytes 131104 | tf_op jit(solution)/shard_map/ppermute | solution.py:21
  28.9 1.2 fusion.26
  30.7 2.9 %fusion.6 = f32[16,16]{0,1:T(8,128)S(1)} fusion(f32[8,32768]{1,0:T(8,128)S(1)} %bitcast.94, f32[8,32768]{1,0:T(8,128)S(1)} %bitcast.92), kind=kOutput, calls=%fused_computation.7 | convolution fusion | flops 101187584 | bytes 2098176 | tf_op jit(solution)/shard_map/dot_general | solution.py:52
  33.5 10.3 %psum.56 = f32[16,16]{0,1:T(8,128)S(1)} all-reduce(f32[16,16]{0,1:T(8,128)S(1)} %fusion.6), channel_id=1, replica_groups=mesh['gx'=4,'gy_0'=4,'gy_1'=2,'gz'=8] {'gx'}, use_global_device_ids=true, to_apply=%region_0.1 | all-reduce | flops 256 | bytes 2048 | tf_op jit(solution)/shard_map/psum | solution.py:34
  43.8 8.8 %psum.57 = f32[16,16]{0,1:T(8,128)S(1)} all-reduce(f32[16,16]{0,1:T(8,128)S(1)} %psum.56), channel_id=1, replica_groups=mesh['gx'=4,'gy_0'=4,'gy_1'=2,'gz'=8] {'gy_0'}, use_global_device_ids=true, to_apply=%region_1.2 | all-reduce | flops 256 | bytes 2048 | tf_op jit(solution)/shard_map/psum | solution.py:34
  52.6 2.5 %psum.58 = f32[16,16]{0,1:T(8,128)S(1)} all-reduce(f32[16,16]{0,1:T(8,128)S(1)} %psum.57), channel_id=1, replica_groups=mesh['gx'=4,'gy_0'=4,'gy_1'=2,'gz'=8] {'gy_1'}, use_global_device_ids=true, to_apply=%region_2.3 | all-reduce | flops 256 | bytes 2048 | tf_op jit(solution)/shard_map/psum | solution.py:34
  55.1 19.4 %psum.59 = f32[16,16]{0,1:T(8,128)S(1)} all-reduce(f32[16,16]{0,1:T(8,128)S(1)} %psum.58), channel_id=1, replica_groups=mesh['gx'=4,'gy_0'=4,'gy_1'=2,'gz'=8] {'gz'}, use_global_device_ids=true, to_apply=%region_3.4 | all-reduce | flops 256 | bytes 2048 | tf_op jit(solution)/shard_map/psum | solution.py:34
  74.6 0.7 cholesky.94
  75.3 0.6 compare_reduce_fusion.2
  76.0 0.6 fusion.55
  76.6 0.6 custom-call.17
  77.6 1.5 fusion.62
  79.1 1.5 fusion.61
  81.3 0.7 cholesky.105
  82.0 0.6 compare_reduce_fusion.1
  82.7 0.6 select_bitcast_fusion.1
  83.3 0.6 custom-call.18
  84.2 1.0 convolution_subtract_fusion
  85.2 1.0 fusion.72
  86.3 1.7 fusion.63
  88.0 0.7 fusion.65
  88.8 1.7 collective-permute-start.7
  90.5 0.7 fusion.64
  91.2 1.7 copy.58
  92.8 1.3 collective-permute-start.10
  94.1 2.3 %copy.59 = f32[8,8,32,1]{2,1,3,0:T(8,128)} copy(f32[8,8,32,1]{3,0,2,1:T(8,128)} %get-tuple-element.69) | data formatting | bytes 16384
  96.4 5.1 %collective-permute-start.11 = (f32[8,8,32,1]{2,1,3,0:T(8,128)}, f32[8,8,32,1]{2,1,3,0:T(8,128)}, u32[]{:S(2)}, u32[]{:S(2)}) collective-permute-start(f32[8,8,32,1]{2,1,3,0:T(8,128)} %copy.59), channel_id=1, source_target_pairs={{0,1},{1,2},{2,3},{3,4},{4,5},{5,6},{6,7},{8,9},{9,10},{10,11},{11... | collective-permute-start | bytes 24584 | tf_op jit(solution)/shard_map/ppermute | solution.py:20
  101.5 1.9 %collective-permute-start.8 = (f32[8,8,1,128]{3,2,1,0:T(1,128)}, f32[8,8,1,128]{3,2,1,0:T(1,128)}, u32[]{:S(2)}, u32[]{:S(2)}) collective-permute-start(f32[8,8,1,128]{3,2,1,0:T(1,128)} %get-tuple-element.71), channel_id=1, source_target_pairs={{8,0},{16,8},{24,16},{32,24},{40,32},{48,40},{56,48},{9,1},{17,9},... | collective-permute-start | bytes 98312 | tf_op jit(solution)/shard_map/ppermute | solution.py:21
  103.5 2.4 %collective-permute-start.9 = (f32[8,8,1,128]{3,2,1,0:T(1,128)}, f32[8,8,1,128]{3,2,1,0:T(1,128)}, u32[]{:S(2)}, u32[]{:S(2)}) collective-permute-start(f32[8,8,1,128]{3,2,1,0:T(1,128)} %get-tuple-element.70), channel_id=1, source_target_pairs={{0,8},{8,16},{16,24},{24,32},{32,40},{40,48},{48,56},{1,9},{9,17},... | collective-permute-start | bytes 98312 | tf_op jit(solution)/shard_map/ppermute | solution.py:20
  106.5 0.7 and_reduce_fusion
  107.6 1.5 collective-permute-start.6
  109.1 2.2 %copy.62 = f32[8,8,32,1]{3,2,1,0:T(8,128)} copy(f32[8,8,32,1]{2,1,3,0:T(8,128)} %collective-permute-done.10) | data formatting | bytes 16384
  111.3 2.2 %copy.63 = f32[8,8,32,1]{3,2,1,0:T(8,128)} copy(f32[8,8,32,1]{2,1,3,0:T(8,128)} %collective-permute-done.11) | data formatting | bytes 16384
  113.5 0.8 pad.51
  114.3 0.8 pad.52
  116.6 1.2 fusion.18
  118.4 3.0 %fusion = f32[24,8]{0,1:T(8,128)S(1)} fusion(f32[8,32768]{1,0:T(8,128)S(1)} %bitcast.96, f32[8,32768]{1,0:T(8,128)S(1)} %fusion.72, f32[8,32768]{1,0:T(8,128)S(1)} %fusion.61), kind=kOutput, calls=%fused_computation.1 | convolution fusion | flops 77070336 | bytes 3146496 | tf_op jit(solution)/shard_map/dot_general | solution.py:52
  121.4 10.4 %psum.60 = f32[24,8]{0,1:T(8,128)S(1)} all-reduce(f32[24,8]{0,1:T(8,128)S(1)} %fusion), channel_id=1, replica_groups=mesh['gx'=4,'gy_0'=4,'gy_1'=2,'gz'=8] {'gx'}, use_global_device_ids=true, to_apply=%region_7.10 | all-reduce | flops 192 | bytes 1536 | tf_op jit(solution)/shard_map/psum | solution.py:34
  131.8 10.7 %psum.61 = f32[24,8]{0,1:T(8,128)S(1)} all-reduce(f32[24,8]{0,1:T(8,128)S(1)} %psum.60), channel_id=1, replica_groups=mesh['gx'=4,'gy_0'=4,'gy_1'=2,'gz'=8] {'gy_0'}, use_global_device_ids=true, to_apply=%region_8.11 | all-reduce | flops 192 | bytes 1536 | tf_op jit(solution)/shard_map/psum | solution.py:34
  142.5 2.5 %psum.62 = f32[24,8]{0,1:T(8,128)S(1)} all-reduce(f32[24,8]{0,1:T(8,128)S(1)} %psum.61), channel_id=1, replica_groups=mesh['gx'=4,'gy_0'=4,'gy_1'=2,'gz'=8] {'gy_1'}, use_global_device_ids=true, to_apply=%region_9.12 | all-reduce | flops 192 | bytes 1536 | tf_op jit(solution)/shard_map/psum | solution.py:34
  144.9 15.0 %psum.63 = f32[24,8]{0,1:T(8,128)S(1)} all-reduce(f32[24,8]{0,1:T(8,128)S(1)} %psum.62), channel_id=1, replica_groups=mesh['gx'=4,'gy_0'=4,'gy_1'=2,'gz'=8] {'gz'}, use_global_device_ids=true, to_apply=%region_10.13 | all-reduce | flops 192 | bytes 1536 | tf_op jit(solution)/shard_map/psum | solution.py:34
  160.1 0.7 cholesky.116
  160.9 0.6 compare_reduce_fusion
  161.5 0.6 select_bitcast_fusion
  162.2 2.0 %dynamic-slice_select_fusion = f32[16,8]{0,1:T(8,128)S(1)} fusion(f32[24,16]{0,1:T(8,128)S(1)} %scatter.19, s32[]{:T(128)} %bitcast.8, s32[]{:T(128)} %bitcast.9, f32[24,8]{0,1:T(8,128)S(1)} %psum.63, pred[]{:T(512)} %and_reduce_fusion), kind=kLoop, calls=%fused_computation.105 | loop fusion | flops 128 | bytes 1545 | tf_op jit(solution)/shard_map/select.25
  164.1 1.7 scatter.20
  166.6 1.5 cholesky.41
  168.1 0.6 compare_reduce_fusion.3
  168.7 0.6 fusion.32
  169.4 1.2 custom-call.15
  171.4 1.1 fusion.10
  173.0 1.2 copy.51
  (71 shorter events, 8.5 us)
Async XLA Ops:
  2.3 23.5 %collective-permute-start.1 = (f32[8,1,32,128]{3,2,1,0:T(8,128)}, f32[8,1,32,128]{3,2,1,0:T(8,128)S(1)}, u32[]{:S(2)}, u32[]{:S(2)}) collective-permute-start(f32[8,1,32,128]{3,2,1,0:T(8,128)} %get-tuple-element.79), channel_id=1, source_target_pairs={{0,64},{64,128},{128,192},{1,65},{65,129},{129,193},{2,66},{66,130... | collective-permute-start | bytes 393224 | tf_op jit(solution)/shard_map/ppermute | solution.py:20
  7.6 8.1 %copy-start = (f32[8,8,32,128]{3,2,1,0:T(8,128)S(1)}, f32[8,8,32,128]{3,2,1,0:T(8,128)}, u32[]{:S(2)}) copy-start(f32[8,8,32,128]{3,2,1,0:T(8,128)} %param.15) | copy-start | bytes 3145732
  7.6 12.5 %copy-start.5 = (f32[8,32,128]{2,1,0:T(8,128)S(1)}, f32[8,32,128]{2,1,0:T(8,128)}, u32[]{:S(2)}) copy-start(f32[8,32,128]{2,1,0:T(8,128)} %param.16) | copy-start | bytes 393220
  8.7 12.1 %collective-permute-start.4 = (f32[8,8,32,1]{2,1,3,0:T(8,128)}, f32[8,8,32,1]{2,1,3,0:T(8,128)}, u32[]{:S(2)}, u32[]{:S(2)}) collective-permute-start(f32[8,8,32,1]{2,1,3,0:T(8,128)} %copy.56), channel_id=1, source_target_pairs={{1,0},{2,1},{3,2},{4,3},{5,4},{6,5},{7,6},{9,8},{10,9},{11,10},{12... | collective-permute-start | bytes 24584 | tf_op jit(solution)/shard_map/ppermute | solution.py:21
  11.0 9.8 %copy-start.6 = (f32[8,1,32,128]{3,2,1,0:T(8,128)S(1)}, f32[8,1,32,128]{3,2,1,0:T(8,128)}, u32[]{:S(2)}) copy-start(f32[8,1,32,128]{3,2,1,0:T(8,128)} %get-tuple-element.78) | copy-start | bytes 393220
  11.0 13.3 %collective-permute-start.5 = (f32[8,8,32,1]{2,1,3,0:T(8,128)}, f32[8,8,32,1]{2,1,3,0:T(8,128)S(1)}, u32[]{:S(2)}, u32[]{:S(2)}) collective-permute-start(f32[8,8,32,1]{2,1,3,0:T(8,128)} %copy.57), channel_id=1, source_target_pairs={{0,1},{1,2},{2,3},{3,4},{4,5},{5,6},{6,7},{8,9},{9,10},{10,11},{11... | collective-permute-start | bytes 24584 | tf_op jit(solution)/shard_map/ppermute | solution.py:20
  15.8 10.0 %collective-permute-start.2 = (f32[8,8,1,128]{3,2,1,0:T(1,128)S(1)}, f32[8,8,1,128]{3,2,1,0:T(1,128)S(1)}, u32[]{:S(2)}, u32[]{:S(2)}) collective-permute-start(f32[8,8,1,128]{3,2,1,0:T(1,128)S(1)} %get-tuple-element.77), channel_id=1, source_target_pairs={{8,0},{16,8},{24,16},{32,24},{40,32},{48,40},{56,48},{9,1},{17,9},... | collective-permute-start | bytes 98312 | tf_op jit(solution)/shard_map/ppermute | solution.py:21
  17.7 8.1 %collective-permute-start.3 = (f32[8,8,1,128]{3,2,1,0:T(1,128)S(1)}, f32[8,8,1,128]{3,2,1,0:T(1,128)S(1)}, u32[]{:S(2)}, u32[]{:S(2)}) collective-permute-start(f32[8,8,1,128]{3,2,1,0:T(1,128)S(1)} %get-tuple-element.76), channel_id=1, source_target_pairs={{0,8},{8,16},{16,24},{24,32},{32,40},{40,48},{48,56},{1,9},{9,17},... | collective-permute-start | bytes 98312 | tf_op jit(solution)/shard_map/ppermute | solution.py:20
  20.8 8.0 %collective-permute-start = (f32[8,1,32,128]{3,2,1,0:T(8,128)S(1)}, f32[8,1,32,128]{3,2,1,0:T(8,128)S(1)}, u32[]{:S(2)}, u32[]{:S(2)}) collective-permute-start(f32[8,1,32,128]{3,2,1,0:T(8,128)S(1)} %copy-done.6), channel_id=1, source_target_pairs={{64,0},{128,64},{192,128},{65,1},{129,65},{193,129},{66,2},{130,66... | collective-permute-start | bytes 393224 | tf_op jit(solution)/shard_map/ppermute | solution.py:21
  25.8 3.0 %copy-start.2 = (f32[8,8,32,1]{3,2,1,0:T(8,128)S(1)}, f32[8,8,32,1]{3,2,1,0:T(8,128)}, u32[]{:S(2)}) copy-start(f32[8,8,32,1]{3,2,1,0:T(8,128)} %copy.60) | copy-start | bytes 24580
  25.8 3.0 %copy-start.4 = (f32[8,8,32,1]{3,2,1,0:T(8,128)S(1)}, f32[8,8,32,1]{3,2,1,0:T(8,128)}, u32[]{:S(2)}) copy-start(f32[8,8,32,1]{3,2,1,0:T(8,128)} %copy.61) | copy-start | bytes 24580
  88.8 26.3 %collective-permute-start.7 = (f32[8,1,32,128]{3,2,1,0:T(8,128)}, f32[8,1,32,128]{3,2,1,0:T(8,128)S(1)}, u32[]{:S(2)}, u32[]{:S(2)}) collective-permute-start(f32[8,1,32,128]{3,2,1,0:T(8,128)} %get-tuple-element.73), channel_id=1, source_target_pairs={{0,64},{64,128},{128,192},{1,65},{65,129},{129,193},{2,66},{66,130... | collective-permute-start | bytes 393224 | tf_op jit(solution)/shard_map/ppermute | solution.py:20
  92.8 14.7 %collective-permute-start.10 = (f32[8,8,32,1]{2,1,3,0:T(8,128)S(1)}, f32[8,8,32,1]{2,1,3,0:T(8,128)}, u32[]{:S(2)}, u32[]{:S(2)}) collective-permute-start(f32[8,8,32,1]{2,1,3,0:T(8,128)S(1)} %copy.58), channel_id=1, source_target_pairs={{1,0},{2,1},{3,2},{4,3},{5,4},{6,5},{7,6},{9,8},{10,9},{11,10},{12... | collective-permute-start | bytes 24584 | tf_op jit(solution)/shard_map/ppermute | solution.py:21
  96.4 14.9 %collective-permute-start.11 = (f32[8,8,32,1]{2,1,3,0:T(8,128)}, f32[8,8,32,1]{2,1,3,0:T(8,128)}, u32[]{:S(2)}, u32[]{:S(2)}) collective-permute-start(f32[8,8,32,1]{2,1,3,0:T(8,128)} %copy.59), channel_id=1, source_target_pairs={{0,1},{1,2},{2,3},{3,4},{4,5},{5,6},{6,7},{8,9},{9,10},{10,11},{11... | collective-permute-start | bytes 24584 | tf_op jit(solution)/shard_map/ppermute | solution.py:20
  101.5 11.9 %collective-permute-start.8 = (f32[8,8,1,128]{3,2,1,0:T(1,128)}, f32[8,8,1,128]{3,2,1,0:T(1,128)}, u32[]{:S(2)}, u32[]{:S(2)}) collective-permute-start(f32[8,8,1,128]{3,2,1,0:T(1,128)} %get-tuple-element.71), channel_id=1, source_target_pairs={{8,0},{16,8},{24,16},{32,24},{40,32},{48,40},{56,48},{9,1},{17,9},... | collective-permute-start | bytes 98312 | tf_op jit(solution)/shard_map/ppermute | solution.py:21
  103.5 10.8 %collective-permute-start.9 = (f32[8,8,1,128]{3,2,1,0:T(1,128)}, f32[8,8,1,128]{3,2,1,0:T(1,128)}, u32[]{:S(2)}, u32[]{:S(2)}) collective-permute-start(f32[8,8,1,128]{3,2,1,0:T(1,128)} %get-tuple-element.70), channel_id=1, source_target_pairs={{0,8},{8,16},{16,24},{24,32},{32,40},{40,48},{48,56},{1,9},{9,17},... | collective-permute-start | bytes 98312 | tf_op jit(solution)/shard_map/ppermute | solution.py:20
  107.6 8.2 %collective-permute-start.6 = (f32[8,1,32,128]{3,2,1,0:T(8,128)}, f32[8,1,32,128]{3,2,1,0:T(8,128)S(1)}, u32[]{:S(2)}, u32[]{:S(2)}) collective-permute-start(f32[8,1,32,128]{3,2,1,0:T(8,128)} %get-tuple-element.72), channel_id=1, source_target_pairs={{64,0},{128,64},{192,128},{65,1},{129,65},{193,129},{66,2},{130,66... | collective-permute-start | bytes 393224 | tf_op jit(solution)/shard_map/ppermute | solution.py:21
  115.1 1.2 copy-start.1
  115.1 1.5 copy-start.3
where the time goes:
time: 175 us; the launch traced here: 174 us
  blocking collectives  79.4 us (45%)
  local copies, waits for them, and re-layouts  30.8 us (18%)
  starting transfers between devices  28.9 us (17%)
  other arithmetic  16.5 us (9%)
  matrix products  14.1 us (8%)
  waiting for transfers between devices  3.37 us (2%)
    psum x8, blocking collectives, by_axis(): value = lax.psum(value, axis)  79.4 us
    ppermute x6, starting transfers between devices, padded_2(): lax.ppermute(last, axis, up)  19.7 us
    unnamed x30, local copies, waits for them, and re-layouts  18.2 us
    dot_general x16, matrix products, small_dot(): return jnp.dot(left, right, precision=lax.Precision.HIGHEST)  13.3 us
    ppermute x6, starting transfers between devices, padded_2(): lax.ppermute(leading, axis, [(b, a) for a, b in up])  9.2 us
    slice x4, local copies, waits for them, and re-layouts, padded_2(): leading = lax.slice_in_dim(value, 0, width, axis=dim)  6.01 us
    another operation x5, other arithmetic  3.95 us
  transfers between devices with their start and end apart: 12, of which 2 were waited for; matrix products, arithmetic and copies ran while one was open for 12% of the time, Pallas kernels for 0%

commit v1 on v0

--- a/solution.py
+++ b/solution.py
@@ -3,10 +3,16 @@
 from jax import lax
 from jax.sharding import Mesh
 from jax.sharding import PartitionSpec as P
+from jax.lax import all_gather
 
 ITERS = 2
 GX_GY_GZ = ("gx", "gy_0", "gy_1", "gz")
 GY = ("gy_0", "gy_1")
+
+
+def threads_mark(message, bus_axis):
+    current_value = jnp.sum(all_gather(message, axis_name=bus_axis), axis=0)
+    return current_value
 
 
 def padded_2(value, sides, width):
@@ -31,7 +37,7 @@
 
 def by_axis(value, axes):
     for axis in axes:
-        value = lax.psum(value, axis)
+        value = threads_mark(value, axis)
     return value
 
 

time: 175 us -> 205 us (1.17)
  blocking collectives: 79.4 us -> 107 us
    all_gather x0 -> x8, blocking collectives: none -> 107 us  [threads_mark(): current_value = jnp.sum(all_gather(message, axis_name=bus_axis), axis=0)]
    psum x8 -> x0, blocking collectives: 79.4 us -> none  [by_axis(): value = lax.psum(value, axis)]
    unnamed x30 -> x31, local copies, waits for them, and re-layouts: 18.2 us -> 18.7 us
  transfers between devices with their start and end apart: 12 -> 12, of which waited for: 2 -> 1; matrix products, arithmetic and copies ran while one was open for 12% -> 10% of each run, Pallas kernels for 0% -> 0%
where the time goes in v1:
time: 205 us; the launch traced here: 203 us
  blocking collectives  107 us (52%)
  local copies, waits for them, and re-layouts  31.2 us (15%)
  starting transfers between devices  30.3 us (15%)
  other arithmetic  16.6 us (8%)
  matrix products  13.9 us (7%)
  waiting for transfers between devices  2.93 us (1%)
    all_gather x8, blocking collectives, threads_mark(): current_value = jnp.sum(all_gather(message, axis_name=bus_axis), axis=0)  107 us
    ppermute x6, starting transfers between devices, padded_2(): lax.ppermute(last, axis, up)  21.1 us
    unnamed x31, local copies, waits for them, and re-layouts  18.7 us
    dot_general x16, matrix products, small_dot(): return jnp.dot(left, right, precision=lax.Precision.HIGHEST)  13.2 us
    ppermute x6, starting transfers between devices, padded_2(): lax.ppermute(leading, axis, [(b, a) for a, b in up])  9.2 us
    slice x4, local copies, waits for them, and re-layouts, padded_2(): leading = lax.slice_in_dim(value, 0, width, axis=dim)  6 us
  transfers between devices with their start and end apart: 12, of which 1 were waited for; matrix products, arithmetic and copies ran while one was open for 10% of the time, Pallas kernels for 0%

profile of v1, /device:TPU:8, one launch (start us, length us, event | category | flops | bytes accessed | tf_op | source)
XLA Modules:
  0.0 202.8 jit_solution(9807192866905583547)
XLA Ops:
  0.6 1.7 fusion.71
  2.3 3.4 %collective-permute-start.1 = (f32[8,1,32,128]{3,2,1,0:T(8,128)}, f32[8,1,32,128]{3,2,1,0:T(8,128)S(1)}, u32[]{:S(2)}, u32[]{:S(2)}) collective-permute-start(f32[8,1,32,128]{3,2,1,0:T(8,128)} %get-tuple-element.81), channel_id=1, source_target_pairs={{0,64},{64,128},{128,192},{1,65},{65,129},{129,193},{2,66},{66,130... | collective-permute-start | bytes 393224 | tf_op jit(solution)/shard_map/ppermute | solution.py:26
  5.7 1.9 fusion.69
  7.7 1.0 copy.80
  8.7 1.3 collective-permute-start.4
  10.0 1.0 copy.81
  11.0 4.7 %collective-permute-start.5 = (f32[8,8,32,1]{2,1,3,0:T(8,128)}, f32[8,8,32,1]{2,1,3,0:T(8,128)S(1)}, u32[]{:S(2)}, u32[]{:S(2)}) collective-permute-start(f32[8,8,32,1]{2,1,3,0:T(8,128)} %copy.81), channel_id=1, source_target_pairs={{0,1},{1,2},{2,3},{3,4},{4,5},{5,6},{6,7},{8,9},{9,10},{10,11},{11... | collective-permute-start | bytes 24584 | tf_op jit(solution)/shard_map/ppermute | solution.py:26
  15.8 1.9 collective-permute-start.2
  17.7 2.4 %collective-permute-start.3 = (f32[8,8,1,128]{3,2,1,0:T(1,128)S(1)}, f32[8,8,1,128]{3,2,1,0:T(1,128)S(1)}, u32[]{:S(2)}, u32[]{:S(2)}) collective-permute-start(f32[8,8,1,128]{3,2,1,0:T(1,128)S(1)} %get-tuple-element.78), channel_id=1, source_target_pairs={{0,8},{8,16},{16,24},{24,32},{32,40},{40,48},{48,56},{1,9},{9,17},... | collective-permute-start | bytes 98312 | tf_op jit(solution)/shard_map/ppermute | solution.py:26
  20.8 1.3 collective-permute-start
  22.1 2.2 %copy.85 = f32[8,8,32,1]{3,2,1,0:T(8,128)} copy(f32[8,8,32,1]{2,1,3,0:T(8,128)} %collective-permute-done.4) | data formatting | bytes 16384
  24.3 1.4 copy.86
  25.9 2.9 %collective-permute-done = f32[8,1,32,128]{3,2,1,0:T(8,128)S(1)} collective-permute-done((f32[8,1,32,128]{3,2,1,0:T(8,128)S(1)}, f32[8,1,32,128]{3,2,1,0:T(8,128)S(1)}, u32[]{:S(2)}, u32[]{:S(2)}) %collective-permute-start) | collective-permute-done | bytes 131104 | tf_op jit(solution)/shard_map/ppermute | solution.py:27
  28.9 1.2 fusion.29
  30.7 2.8 %fusion.6 = f32[16,16]{1,0:T(8,128)S(1)} fusion(f32[8,32768]{1,0:T(8,128)S(1)} %bitcast.103, f32[8,32768]{1,0:T(8,128)S(1)} %bitcast.101), kind=kOutput, calls=%fused_computation.7 | convolution fusion | flops 101187584 | bytes 2098176 | tf_op jit(solution)/shard_map/dot_general | solution.py:58
  33.4 12.0 %all-gather = f32[64,16]{1,0:T(8,128)S(1)} all-gather(f32[16,16]{1,0:T(8,128)S(1)} %fusion.6), channel_id=2, replica_groups=mesh['gx'=4,'gy_0'=4,'gy_1'=2,'gz'=8] {'gx'}, dimensions={0}, use_global_device_ids=true | all-gather | bytes 5120 | tf_op jit(solution)/shard_map/all_gather | solution.py:14
  45.4 12.1 %all-gather.1 = f32[64,16]{1,0:T(8,128)S(1)} all-gather(f32[16,16]{1,0:T(8,128)S(1)} %reduce_sum.81), channel_id=3, replica_groups=mesh['gx'=4,'gy_0'=4,'gy_1'=2,'gz'=8] {'gy_0'}, dimensions={0}, use_global_device_ids=true | all-gather | bytes 5120 | tf_op jit(solution)/shard_map/all_gather | solution.py:14
  57.5 1.8 all-gather.2
  59.3 29.2 %all-gather.3 = f32[128,16]{1,0:T(8,128)S(1)} all-gather(f32[16,16]{1,0:T(8,128)S(1)} %reduce_sum.83), channel_id=5, replica_groups=mesh['gx'=4,'gy_0'=4,'gy_1'=2,'gz'=8] {'gz'}, dimensions={0}, use_global_device_ids=true | all-gather | bytes 9216 | tf_op jit(solution)/shard_map/all_gather | solution.py:14
  88.6 0.7 cholesky.94
  89.4 0.6 compare_reduce_fusion.2
  90.0 0.6 fusion.58
  90.7 0.6 custom-call.17
  91.7 1.5 fusion.65
  93.2 1.5 fusion.64
  95.4 0.7 cholesky.105
  96.1 0.6 compare_reduce_fusion.1
  96.8 0.6 select_bitcast_fusion.1
  98.2 1.0 convolution_subtract_fusion
  99.2 1.0 fusion.75
  100.4 1.7 fusion.66
  102.1 0.7 fusion.68
  102.8 3.1 %collective-permute-start.7 = (f32[8,1,32,128]{3,2,1,0:T(8,128)}, f32[8,1,32,128]{3,2,1,0:T(8,128)S(1)}, u32[]{:S(2)}, u32[]{:S(2)}) collective-permute-start(f32[8,1,32,128]{3,2,1,0:T(8,128)} %get-tuple-element.75), channel_id=1, source_target_pairs={{0,64},{64,128},{128,192},{1,65},{65,129},{129,193},{2,66},{66,130... | collective-permute-start | bytes 393224 | tf_op jit(solution)/shard_map/ppermute | solution.py:26
  105.9 0.7 fusion.67
  106.6 1.7 copy.83
  108.3 1.3 collective-permute-start.10
  109.6 2.3 %copy.84 = f32[8,8,32,1]{2,1,3,0:T(8,128)} copy(f32[8,8,32,1]{3,0,2,1:T(8,128)} %get-tuple-element.71) | data formatting | bytes 16384
  111.8 5.1 %collective-permute-start.11 = (f32[8,8,32,1]{2,1,3,0:T(8,128)}, f32[8,8,32,1]{2,1,3,0:T(8,128)}, u32[]{:S(2)}, u32[]{:S(2)}) collective-permute-start(f32[8,8,32,1]{2,1,3,0:T(8,128)} %copy.84), channel_id=1, source_target_pairs={{0,1},{1,2},{2,3},{3,4},{4,5},{5,6},{6,7},{8,9},{9,10},{10,11},{11... | collective-permute-start | bytes 24584 | tf_op jit(solution)/shard_map/ppermute | solution.py:26
  117.0 1.9 collective-permute-start.8
  118.9 2.4 %collective-permute-start.9 = (f32[8,8,1,128]{3,2,1,0:T(1,128)}, f32[8,8,1,128]{3,2,1,0:T(1,128)}, u32[]{:S(2)}, u32[]{:S(2)}) collective-permute-start(f32[8,8,1,128]{3,2,1,0:T(1,128)} %get-tuple-element.72), channel_id=1, source_target_pairs={{0,8},{8,16},{16,24},{24,32},{32,40},{40,48},{48,56},{1,9},{9,17},... | collective-permute-start | bytes 98312 | tf_op jit(solution)/shard_map/ppermute | solution.py:26
  121.9 0.7 and_reduce_fusion
  123.0 1.5 collective-permute-start.6
  124.5 2.2 %copy.87 = f32[8,8,32,1]{3,2,1,0:T(8,128)} copy(f32[8,8,32,1]{2,1,3,0:T(8,128)} %collective-permute-done.10) | data formatting | bytes 16384
  126.7 2.2 %copy.88 = f32[8,8,32,1]{3,2,1,0:T(8,128)} copy(f32[8,8,32,1]{2,1,3,0:T(8,128)} %collective-permute-done.11) | data formatting | bytes 16384
  128.9 0.8 pad.51
  129.7 0.8 pad.52
  130.8 1.0 copy-done.1
  132.1 1.2 fusion.21
  133.8 3.0 %fusion.14 = f32[1,24,8]{1,2,0:T(8,128)S(1)} fusion(f32[8,32768]{1,0:T(8,128)S(1)} %bitcast.105, f32[8,32768]{1,0:T(8,128)S(1)} %fusion.75, f32[8,32768]{1,0:T(8,128)S(1)} %fusion.64), kind=kOutput, calls=%fused_computation.15 | convolution fusion | flops 77070336 | bytes 3146496 | tf_op jit(solution)/shard_map/dot_general | solution.py:58
  136.9 12.6 %all-gather.8 = f32[4,24,8]{1,2,0:T(8,128)S(1)} all-gather(f32[1,24,8]{1,2,0:T(8,128)S(1)} %fusion.14), channel_id=6, replica_groups=mesh['gx'=4,'gy_0'=4,'gy_1'=2,'gz'=8] {'gx'}, dimensions={0}, use_global_device_ids=true | all-gather | bytes 3840 | tf_op jit(solution)/shard_map/all_gather | solution.py:14
  149.5 12.6 %all-gather.9 = f32[4,24,8]{1,2,0:T(8,128)S(1)} all-gather(f32[1,24,8]{1,2,0:T(8,128)S(1)} %bitcast.111), channel_id=7, replica_groups=mesh['gx'=4,'gy_0'=4,'gy_1'=2,'gz'=8] {'gy_0'}, dimensions={0}, use_global_device_ids=true | all-gather | bytes 3840 | tf_op jit(solution)/shard_map/all_gather | solution.py:14
  162.1 1.8 all-gather.10
  163.9 24.7 %all-gather.11 = f32[8,24,8]{1,2,0:T(8,128)S(1)} all-gather(f32[1,24,8]{1,2,0:T(8,128)S(1)} %bitcast.110), channel_id=9, replica_groups=mesh['gx'=4,'gy_0'=4,'gy_1'=2,'gz'=8] {'gz'}, dimensions={0}, use_global_device_ids=true | all-gather | bytes 6912 | tf_op jit(solution)/shard_map/all_gather | solution.py:14
  188.8 0.7 cholesky.116
  189.6 0.6 compare_reduce_fusion
  190.2 0.6 select_bitcast_fusion
  190.9 2.0 dynamic-slice_select_fusion
  192.9 1.7 scatter.20
  195.3 1.5 cholesky.41
  196.8 0.6 compare_reduce_fusion.3
  197.4 0.6 fusion.35
  198.1 1.2 custom-call.15
  200.0 1.1 fusion.10
  201.6 1.2 copy.76
  (79 shorter events, 8.2 us)
Async XLA Ops:
  2.3 23.5 %collective-permute-start.1 = (f32[8,1,32,128]{3,2,1,0:T(8,128)}, f32[8,1,32,128]{3,2,1,0:T(8,128)S(1)}, u32[]{:S(2)}, u32[]{:S(2)}) collective-permute-start(f32[8,1,32,128]{3,2,1,0:T(8,128)} %get-tuple-element.81), channel_id=1, source_target_pairs={{0,64},{64,128},{128,192},{1,65},{65,129},{129,193},{2,66},{66,130... | collective-permute-start | bytes 393224 | tf_op jit(solution)/shard_map/ppermute | solution.py:26
  7.6 8.1 %copy-start = (f32[8,8,32,128]{3,2,1,0:T(8,128)S(1)}, f32[8,8,32,128]{3,2,1,0:T(8,128)}, u32[]{:S(2)}) copy-start(f32[8,8,32,128]{3,2,1,0:T(8,128)} %param.15) | copy-start | bytes 3145732
  7.6 12.5 %copy-start.5 = (f32[8,32,128]{2,1,0:T(8,128)S(1)}, f32[8,32,128]{2,1,0:T(8,128)}, u32[]{:S(2)}) copy-start(f32[8,32,128]{2,1,0:T(8,128)} %param.16) | copy-start | bytes 393220
  8.7 12.1 %collective-permute-start.4 = (f32[8,8,32,1]{2,1,3,0:T(8,128)}, f32[8,8,32,1]{2,1,3,0:T(8,128)}, u32[]{:S(2)}, u32[]{:S(2)}) collective-permute-start(f32[8,8,32,1]{2,1,3,0:T(8,128)} %copy.80), channel_id=1, source_target_pairs={{1,0},{2,1},{3,2},{4,3},{5,4},{6,5},{7,6},{9,8},{10,9},{11,10},{12... | collective-permute-start | bytes 24584 | tf_op jit(solution)/shard_map/ppermute | solution.py:27
  11.0 9.8 %copy-start.6 = (f32[8,1,32,128]{3,2,1,0:T(8,128)S(1)}, f32[8,1,32,128]{3,2,1,0:T(8,128)}, u32[]{:S(2)}) copy-start(f32[8,1,32,128]{3,2,1,0:T(8,128)} %get-tuple-element.80) | copy-start | bytes 393220
  11.0 13.3 %collective-permute-start.5 = (f32[8,8,32,1]{2,1,3,0:T(8,128)}, f32[8,8,32,1]{2,1,3,0:T(8,128)S(1)}, u32[]{:S(2)}, u32[]{:S(2)}) collective-permute-start(f32[8,8,32,1]{2,1,3,0:T(8,128)} %copy.81), channel_id=1, source_target_pairs={{0,1},{1,2},{2,3},{3,4},{4,5},{5,6},{6,7},{8,9},{9,10},{10,11},{11... | collective-permute-start | bytes 24584 | tf_op jit(solution)/shard_map/ppermute | solution.py:26
  15.8 10.0 %collective-permute-start.2 = (f32[8,8,1,128]{3,2,1,0:T(1,128)S(1)}, f32[8,8,1,128]{3,2,1,0:T(1,128)S(1)}, u32[]{:S(2)}, u32[]{:S(2)}) collective-permute-start(f32[8,8,1,128]{3,2,1,0:T(1,128)S(1)} %get-tuple-element.79), channel_id=1, source_target_pairs={{8,0},{16,8},{24,16},{32,24},{40,32},{48,40},{56,48},{9,1},{17,9},... | collective-permute-start | bytes 98312 | tf_op jit(solution)/shard_map/ppermute | solution.py:27
  17.7 8.1 %collective-permute-start.3 = (f32[8,8,1,128]{3,2,1,0:T(1,128)S(1)}, f32[8,8,1,128]{3,2,1,0:T(1,128)S(1)}, u32[]{:S(2)}, u32[]{:S(2)}) collective-permute-start(f32[8,8,1,128]{3,2,1,0:T(1,128)S(1)} %get-tuple-element.78), channel_id=1, source_target_pairs={{0,8},{8,16},{16,24},{24,32},{32,40},{40,48},{48,56},{1,9},{9,17},... | collective-permute-start | bytes 98312 | tf_op jit(solution)/shard_map/ppermute | solution.py:26
  20.8 8.0 %collective-permute-start = (f32[8,1,32,128]{3,2,1,0:T(8,128)S(1)}, f32[8,1,32,128]{3,2,1,0:T(8,128)S(1)}, u32[]{:S(2)}, u32[]{:S(2)}) collective-permute-start(f32[8,1,32,128]{3,2,1,0:T(8,128)S(1)} %copy-done.6), channel_id=1, source_target_pairs={{64,0},{128,64},{192,128},{65,1},{129,65},{193,129},{66,2},{130,66... | collective-permute-start | bytes 393224 | tf_op jit(solution)/shard_map/ppermute | solution.py:27
  25.8 3.0 %copy-start.2 = (f32[8,8,32,1]{3,2,1,0:T(8,128)S(1)}, f32[8,8,32,1]{3,2,1,0:T(8,128)}, u32[]{:S(2)}) copy-start(f32[8,8,32,1]{3,2,1,0:T(8,128)} %copy.85) | copy-start | bytes 24580
  25.8 3.0 %copy-start.4 = (f32[8,8,32,1]{3,2,1,0:T(8,128)S(1)}, f32[8,8,32,1]{3,2,1,0:T(8,128)}, u32[]{:S(2)}) copy-start(f32[8,8,32,1]{3,2,1,0:T(8,128)} %copy.86) | copy-start | bytes 24580
  102.8 27.7 %collective-permute-start.7 = (f32[8,1,32,128]{3,2,1,0:T(8,128)}, f32[8,1,32,128]{3,2,1,0:T(8,128)S(1)}, u32[]{:S(2)}, u32[]{:S(2)}) collective-permute-start(f32[8,1,32,128]{3,2,1,0:T(8,128)} %get-tuple-element.75), channel_id=1, source_target_pairs={{0,64},{64,128},{128,192},{1,65},{65,129},{129,193},{2,66},{66,130... | collective-permute-start | bytes 393224 | tf_op jit(solution)/shard_map/ppermute | solution.py:26
  108.3 14.7 %collective-permute-start.10 = (f32[8,8,32,1]{2,1,3,0:T(8,128)S(1)}, f32[8,8,32,1]{2,1,3,0:T(8,128)}, u32[]{:S(2)}, u32[]{:S(2)}) collective-permute-start(f32[8,8,32,1]{2,1,3,0:T(8,128)S(1)} %copy.83), channel_id=1, source_target_pairs={{1,0},{2,1},{3,2},{4,3},{5,4},{6,5},{7,6},{9,8},{10,9},{11,10},{12... | collective-permute-start | bytes 24584 | tf_op jit(solution)/shard_map/ppermute | solution.py:27
  111.8 14.9 %collective-permute-start.11 = (f32[8,8,32,1]{2,1,3,0:T(8,128)}, f32[8,8,32,1]{2,1,3,0:T(8,128)}, u32[]{:S(2)}, u32[]{:S(2)}) collective-permute-start(f32[8,8,32,1]{2,1,3,0:T(8,128)} %copy.84), channel_id=1, source_target_pairs={{0,1},{1,2},{2,3},{3,4},{4,5},{5,6},{6,7},{8,9},{9,10},{10,11},{11... | collective-permute-start | bytes 24584 | tf_op jit(solution)/shard_map/ppermute | solution.py:26
  117.0 11.9 %collective-permute-start.8 = (f32[8,8,1,128]{3,2,1,0:T(1,128)}, f32[8,8,1,128]{3,2,1,0:T(1,128)}, u32[]{:S(2)}, u32[]{:S(2)}) collective-permute-start(f32[8,8,1,128]{3,2,1,0:T(1,128)} %get-tuple-element.73), channel_id=1, source_target_pairs={{8,0},{16,8},{24,16},{32,24},{40,32},{48,40},{56,48},{9,1},{17,9},... | collective-permute-start | bytes 98312 | tf_op jit(solution)/shard_map/ppermute | solution.py:27
  118.9 10.8 %collective-permute-start.9 = (f32[8,8,1,128]{3,2,1,0:T(1,128)}, f32[8,8,1,128]{3,2,1,0:T(1,128)}, u32[]{:S(2)}, u32[]{:S(2)}) collective-permute-start(f32[8,8,1,128]{3,2,1,0:T(1,128)} %get-tuple-element.72), channel_id=1, source_target_pairs={{0,8},{8,16},{16,24},{24,32},{32,40},{40,48},{48,56},{1,9},{9,17},... | collective-permute-start | bytes 98312 | tf_op jit(solution)/shard_map/ppermute | solution.py:26
  123.0 7.7 %collective-permute-start.6 = (f32[8,1,32,128]{3,2,1,0:T(8,128)}, f32[8,1,32,128]{3,2,1,0:T(8,128)S(1)}, u32[]{:S(2)}, u32[]{:S(2)}) collective-permute-start(f32[8,1,32,128]{3,2,1,0:T(8,128)} %get-tuple-element.74), channel_id=1, source_target_pairs={{64,0},{128,64},{192,128},{65,1},{129,65},{193,129},{66,2},{130,66... | collective-permute-start | bytes 393224 | tf_op jit(solution)/shard_map/ppermute | solution.py:27
  130.5 1.2 copy-start.1
  130.5 1.5 copy-start.3
